TPU v7x, 32 devices: a whole 2x2x4 slice. The times are simulated.
32 devices in a mesh: rep: 4 (over z), gy: 2 (over y), gz: 4 (over x, core).
Axes of the slice: x: 2, y: 2, z: 4, core: 2. Of those that a mesh axis runs over, the one named last changes fastest.
Arguments:
- charges: float32 [1024, 256, 128], P(('rep', 'gz'), 'gy'), may hold values from -6 to 6
- green: float32 [256, 256, 128], P('rep', ('gy', 'gz')), may hold values from 0.1 to 3
Outputs:
- potential: float32 [1024, 256, 128], P(('rep', 'gz'), 'gy')
All inputs are finite; a program needn't handle non-finite values.
Results may differ from a plain program's by a relative error of at most 0.00007.
Values sent between devices are 32-bit elements; how exact they have to be, the bound alone decides.
A program may use at most 64 MiB of HBM per device.

v0:
```python
import functools
import math

import jax
import jax.numpy as jnp
import numpy as np
from jax import lax
from jax.experimental import pallas as pl
from jax.experimental.pallas import tpu as pltpu
from jax.sharding import PartitionSpec as P

NG = 256
NZ = 128


two_pi = 2.0 * math.pi
highest = lax.Precision.HIGHEST


def tables(length, rows_index, cols_index):
    phase = rows_index[:, None] * cols_index[None, :] % length
    angle = phase.astype(jnp.float32) * (two_pi / length)
    return (jnp.cos(angle), jnp.sin(angle))


def reflect(values):
    return jnp.roll(jnp.flip(values, (1, 2)), (1, 1), axis=(1, 2))


def slab_plan(charges, green):
    gy_count = lax.axis_size("gy")
    gz_count = lax.axis_size("gz")
    groups = gy_count * gz_count
    half = NZ // 2
    per_device = half // groups
    col_block = charges.shape[1]
    depth = jnp.arange(NZ, dtype=jnp.int32)
    bins = jnp.arange(half, dtype=jnp.int32)
    indices = jnp.arange(NG, dtype=jnp.int32)
    cos_depth, sin_depth = tables(NZ, depth, bins)
    alternate = (1 - 2 * (depth % 2)).astype(jnp.float32)
    sin_packed = jnp.where(bins[None, :] == 0, -alternate[:, None], sin_depth)
    spec_re = jnp.einsum("xyz,zk->kxy", charges, cos_depth, precision=highest)
    spec_im = -jnp.einsum("xyz,zk->kxy", charges, sin_packed, precision=highest)
    own = jnp.moveaxis(green[:, :, :half], 2, 0)
    mirror = jnp.concatenate(
        [green[:, :, half : half + 1], jnp.flip(green[:, :, half + 1 :], 2)], axis=2
    )
    mirror = jnp.moveaxis(mirror, 2, 0)
    own, mirror = (
        lax.all_to_all(own, ("gy", "gz"), split_axis=0, concat_axis=2, tiled=True),
        lax.all_to_all(mirror, ("gy", "gz"), split_axis=0, concat_axis=2, tiled=True),
    )
    own, mirror = (
        lax.all_gather(own, "rep", axis=1, tiled=True),
        lax.all_gather(mirror, "rep", axis=1, tiled=True),
    )
    plane_re, plane_im = (
        lax.all_to_all(spec_re, ("gy", "gz"), split_axis=0, concat_axis=1, tiled=True),
        lax.all_to_all(spec_im, ("gy", "gz"), split_axis=0, concat_axis=1, tiled=True),
    )
    plane_re = plane_re.reshape(per_device, gy_count, NG, col_block)
    plane_im = plane_im.reshape(per_device, gy_count, NG, col_block)
    cos_plain, sin_plain = tables(NG, indices, indices)
    wide_cos = cos_plain.reshape(NG, gy_count, col_block)
    wide_sin = sin_plain.reshape(NG, gy_count, col_block)

    def second_in(matrix, values):
        return jnp.einsum("kgc,bgxc->bxk", matrix, values, precision=highest)

    def first_in(matrix, values):
        return jnp.einsum("kx,bxj->bkj", matrix, values, precision=highest)

    inner_re = second_in(wide_cos, plane_re) + second_in(wide_sin, plane_im)
    inner_im = second_in(wide_cos, plane_im) - second_in(wide_sin, plane_re)
    freq_re = first_in(cos_plain, inner_re) + first_in(sin_plain, inner_im)
    freq_im = first_in(cos_plain, inner_im) - first_in(sin_plain, inner_re)
    slot = lax.axis_index("gy") * gz_count + lax.axis_index("gz")
    packed = ((slot == 0) & (jnp.arange(per_device) == 0))[:, None, None]
    plain_gain = 0.5 * (own + reflect(mirror))
    first_gain = jnp.where(packed, 0.5 * (own + reflect(own)), plain_gain)
    second_gain = jnp.where(packed, 0.5 * (mirror + reflect(mirror)), plain_gain)
    mean_gain = 0.5 * (first_gain + second_gain)
    odd_gain = 0.5 * (first_gain - second_gain)
    prod_re = freq_re * mean_gain + reflect(freq_re) * odd_gain
    prod_im = freq_im * mean_gain - reflect(freq_im) * odd_gain
    undo_re = first_in(cos_plain, prod_re) - first_in(sin_plain, prod_im)
    undo_im = first_in(sin_plain, prod_re) + first_in(cos_plain, prod_im)

    def second_out(matrix, values):
        return jnp.einsum("kgc,bxk->bgxc", matrix, values, precision=highest)

    cells_re = second_out(wide_cos, undo_re) - second_out(wide_sin, undo_im)
    cells_im = second_out(wide_sin, undo_re) + second_out(wide_cos, undo_im)
    cells_re = cells_re.reshape(per_device, gy_count * NG, col_block)
    cells_im = cells_im.reshape(per_device, gy_count * NG, col_block)
    home_re, home_im = (
        lax.all_to_all(cells_re, ("gy", "gz"), split_axis=1, concat_axis=0, tiled=True),
        lax.all_to_all(cells_im, ("gy", "gz"), split_axis=1, concat_axis=0, tiled=True),
    )
    weight = jnp.where(bins == 0, 1.0, 2.0).astype(jnp.float32)
    cos_back = (cos_depth * weight[None, :]).T
    sin_back = jnp.where(bins[:, None] == 0, alternate[None, :], -2.0 * sin_depth.T)
    result_field = jnp.einsum("kxy,kz->xyz", home_re, cos_back, precision=highest)
    result_field = result_field + jnp.einsum("kxy,kz->xyz", home_im, sin_back, precision=highest)
    return result_field / (NG * NG * NZ)


f32 = jnp.float32
bf16 = jnp.bfloat16
MESH = pl.DeviceIdType.MESH
PARTS = 2


def split(values):
    high = values.astype(bf16)
    return high, (values - high.astype(f32)).astype(bf16)


def stacked_table(table, axis):
    rounded = table.astype(jnp.bfloat16)
    return jnp.asarray(np.stack([rounded, (table - rounded.astype(np.float64)).astype(jnp.bfloat16)], axis=axis))


def split_table(table):
    rounded = table.astype(jnp.bfloat16)
    high = jnp.asarray(rounded)
    low = jnp.asarray((table - rounded.astype(np.float64)).astype(jnp.bfloat16))
    return high, low


def dot(left, right, dims=((1,), (0,))):
    return lax.dot_general(left, right, (dims, ((), ())), preferred_element_type=f32)


def dot_table(values, table_high, table_low, dims=((1,), (0,))):
    high, low = split(values)
    return dot(high, table_high, dims) + (dot(low, table_high, dims) + dot(high, table_low, dims))


def table_dot(table_high, table_low, values, dims=((1,), (0,))):
    high, low = split(values)
    return dot(table_high, high, dims) + (dot(table_high, low, dims) + dot(table_low, high, dims))


def depth_tables(length, groups, bins_each):
    per_part = bins_each // PARTS
    forward, back = [], []
    z = np.arange(length)
    alternate = 1.0 - 2.0 * (z % 2)
    for start in range(0, groups * bins_each, per_part):
        for imaginary in (False, True):
            for k in range(start, start + per_part):
                angle = 2.0 * np.pi * ((k * z) % length) / length
                if k == 0:
                    forward.append(alternate if imaginary else np.ones(length))
                    back.append(alternate if imaginary else np.ones(length))
                else:
                    forward.append(-np.sin(angle) if imaginary else np.cos(angle))
                    back.append(-2.0 * np.sin(angle) if imaginary else 2.0 * np.cos(angle))
    return np.stack(forward), np.stack(back)


def depth_in(table, cells, out):
    groups, parts, _, cols = out.shape
    rows, depth, step = cells.shape[0], cells.shape[2], 8

    def body(i, carry):
        values = cells[pl.ds(i * step, step)].reshape(step * cols, depth)
        result = table_dot(table[0], table[1], values, ((1,), (1,)))
        for row in range(step):
            piece = result[:, row * cols : (row + 1) * cols]
            at = pl.multiple_of(i * (step * 8) + row * 8, 8)
            out[:, :, pl.ds(at, 8), :] = piece.reshape(groups, parts, 8, cols)
        return carry

    lax.fori_loop(0, rows // step, body, 0)


def depth_out_kernel(high_ref, low_ref, spec_ref, out_ref):
    rows, cols, depth = out_ref.shape
    pieces = [
        spec_ref[:, :, row * 8 : (row + 1) * 8, :].reshape(high_ref.shape[0], cols) for row in range(rows)
    ]
    values = jnp.concatenate(pieces, axis=1)
    result = dot_table(values, high_ref[...], low_ref[...], ((0,), (0,)))
    out_ref[...] = result.reshape(rows, cols, depth)


def pick_green(pick_ref, green_ref, out_ref):
    groups, parts, _, _ = out_ref.shape
    count = green_ref.shape[0] // 64
    rest = jnp.concatenate([green_ref[pl.ds(k2, 64, stride=count), :] for k2 in range(count)], axis=0)
    result = None
    for _ in range(3):
        high = rest.astype(bf16)
        rest = rest - high.astype(f32)
        term = dot(pick_ref[...], high, ((1,), (1,)))
        result = term if result is None else result + term
    size = groups * parts * 8
    first_lanes = lax.broadcasted_iota(jnp.int32, (size, 128), 1) < 64
    first_rows = lax.rem(lax.broadcasted_iota(jnp.int32, (size, 128), 0), 8) < 4
    for pair in range(count // 2):
        own = result[:size, pair * 128 : (pair + 1) * 128]
        mirror = result[size:, pair * 128 : (pair + 1) * 128]
        even = jnp.where(first_lanes, own, pltpu.roll(mirror, 64, 1))
        odd = jnp.where(first_lanes, pltpu.roll(own, 64, 1), mirror)
        out_ref[:, :, pair * 8 : (pair + 1) * 8, :] = jnp.where(first_rows, even, odd).reshape(groups, parts, 8, 128)


def planes_kernel(
    gy_count, gz_count, reps,
    cells_in, green_in, pick_in, depth_table, waves_ref, flips_ref, home_ref,
    cells_ref, field_ref, pick_ref, depth_ref, gains_ref, spec_ref,
    planes, green, freq, tables, flips,
    fwd_send, fwd_recv, back_send, back_recv, green_send, green_recv, right_send, left_send, line_recv, own_sem, table_sem, in_sem,
):
    groups = gy_count * gz_count
    rep, gy, gz = lax.axis_index("rep"), lax.axis_index("gy"), lax.axis_index("gz")
    slot = gy * gz_count + gz
    rows = spec_ref.shape[2] // 8
    ng = flips_ref.shape[1]
    piece = gains_ref.shape[2]

    def partner(step):
        there_y = lax.rem(gy + step // gz_count, gy_count)
        there_z = lax.rem(gz + step % gz_count, gz_count)
        return there_y * gz_count + there_z, {"rep": rep, "gy": there_y, "gz": there_z}

    def along(step):
        return {"rep": lax.rem(rep + step + reps, reps), "gy": gy, "gz": gz}

    inputs = [
        pltpu.make_async_copy(source, held, in_sem.at[i])
        for i, (source, held) in enumerate((
            (green_in, field_ref), (pick_in, pick_ref), (cells_in, cells_ref), (depth_table, depth_ref)))
    ]
    for copy in inputs:
        copy.start()

    loads = []
    for table, (kind, swap) in enumerate(((1, False), (0, True), (0, False), (2, True))):
        minus, plus = (1, 2) if swap else (2, 1)
        for quadrant, wave in enumerate((0, minus, plus, 0)):
            loads.append(pltpu.make_async_copy(
                waves_ref.at[3 * kind + wave],
                tables.at[table, :, pl.ds(quadrant // 2 * ng, ng), pl.ds(quadrant % 2 * ng, ng)],
                table_sem.at[4 * table + quadrant]))
    loads.append(pltpu.make_async_copy(flips_ref, flips, table_sem.at[16]))
    for load in loads:
        load.start()

    order = sorted(range(1, groups), key=lambda s: (-(s % gz_count), s))

    barrier = pltpu.get_barrier_semaphore()
    for step in order:
        pl.semaphore_signal(barrier, inc=1, device_id=partner(step)[1], device_id_type=MESH)
    for step in (1, -1):
        pl.semaphore_signal(barrier, inc=1, device_id=along(step), device_id_type=MESH)
    for copy in inputs[:2]:
        copy.wait()
    pick_green(pick_ref, field_ref, gains_ref)
    pl.semaphore_wait(barrier, groups + 1)

    def green_copy(step, source, part):
        there, device = partner(step)
        return pltpu.make_async_remote_copy(
            src_ref=gains_ref.at[there, part], dst_ref=green.at[rep, part, pl.ds(source * piece, piece), :],
            send_sem=green_send.at[there, part], recv_sem=green_recv.at[source, part], device_id=device, device_id_type=MESH)

    def fwd_copy(step, source, part):
        there, device = partner(step)
        return pltpu.make_async_remote_copy(
            src_ref=spec_ref.at[there, part], dst_ref=planes.at[source, part],
            send_sem=fwd_send.at[there, part], recv_sem=fwd_recv.at[source, part], device_id=device, device_id_type=MESH)

    def back_copy(step, source, part):
        there, device = partner(step)
        return pltpu.make_async_remote_copy(
            src_ref=planes.at[there, part], dst_ref=home_ref.at[source, part],
            send_sem=back_send.at[there, part], recv_sem=back_recv.at[source, part], device_id=device, device_id_type=MESH)

    def line_copy(block, part, sem, step):
        return pltpu.make_async_remote_copy(
            src_ref=green.at[block, part], dst_ref=green.at[block, part], send_sem=sem.at[part],
            recv_sem=line_recv.at[block, part], device_id=along(step), device_id_type=MESH)

    own_green = [
        pltpu.make_async_copy(
            gains_ref.at[slot, h], green.at[rep, h, pl.ds(slot * piece, piece), :], own_sem.at[PARTS + h])
        for h in range(PARTS)
    ]
    own_planes = [pltpu.make_async_copy(spec_ref.at[slot, h], planes.at[slot, h], own_sem.at[h]) for h in range(PARTS)]
    for part in range(PARTS):
        for step in order:
            green_copy(step, slot, part).start()
    for copy in own_green:
        copy.start()
    for copy in inputs[2:]:
        copy.wait()
    depth_in(depth_ref, cells_ref, spec_ref)
    for copy in own_planes:
        copy.start()

    def line_start(part):
        @pl.when(rep + 1 < reps)
        def _():
            line_copy(rep, part, right_send.at[0], 1).start()

        @pl.when(rep >= 1)
        def _():
            line_copy(rep, part, left_send.at[0], -1).start()

    def relay(hop, part):
        @pl.when(rep >= hop)
        def _():
            line_copy(rep - hop, part, right_send.at[hop], 1).wait_recv()

        @pl.when((rep >= hop) & (rep + 1 < reps))
        def _():
            line_copy(rep - hop, part, right_send.at[hop], 1).start()

        @pl.when(rep + hop < reps)
        def _():
            line_copy(rep + hop, part, left_send.at[hop], -1).wait_recv()

        @pl.when((rep + hop < reps) & (rep >= 1))
        def _():
            line_copy(rep + hop, part, left_send.at[hop], -1).start()

    def load_plane(part, row):
        bands = []
        for y in range(gy_count):
            bands.append(jnp.concatenate(
                [planes[y * gz_count + x, part, pl.ds(row, rows, stride=8), :] for x in range(gz_count)], axis=0))
        return jnp.concatenate(bands, axis=1)

    def forward(part):
        def body(p, carry):
            values = jnp.concatenate([load_plane(part, p), load_plane(part, 4 + p)], axis=1)
            inner = dot_table(values, tables[0, 0], tables[0, 1])
            inner = jnp.concatenate([inner[:, :ng], inner[:, ng:]], axis=0)
            freq[part * 4 + p] = table_dot(tables[1, 0], tables[1, 1], inner)
            return carry

        lax.fori_loop(0, 4, body, 0)

    def reflect_plane(values):
        high, low = split(values)
        turned = dot(flips[0], high) + dot(flips[0], low)
        high, low = split(turned)
        return dot(high, flips[1]) + dot(low, flips[1])

    def backward(part):
        def body(p, carry):
            plane = part * 4 + p
            own, mirror = [], []
            lane = lax.broadcasted_iota(jnp.int32, (ng, 128), 1)
            for r in range(0, reps, 2):
                one, two = (
                    jnp.concatenate([green[q, part, pl.ds(4 * odd + p, ng // 2, stride=8), :] for odd in range(2)], axis=0)
                    for q in (r, r + 1)
                )
                own.append(jnp.where(lane < 64, one, pltpu.roll(two, 64, 1)))
                mirror.append(jnp.where(lane < 64, pltpu.roll(one, 64, 1), two))
            own = jnp.concatenate(own, axis=1).T
            mirror = jnp.concatenate(mirror, axis=1).T
            packed = (slot == 0) & (plane == 0)

            @pl.when(jnp.logical_not(packed))
            def _():
                gain = 0.5 * (own + reflect_plane(mirror))
                freq[plane] = freq[plane] * jnp.concatenate([gain, gain], axis=0)

            @pl.when(packed)
            def _():
                first = 0.5 * (own + reflect_plane(own))
                second = 0.5 * (mirror + reflect_plane(mirror))
                mean, odd = 0.5 * (first + second), 0.5 * (first - second)
                real, imag = freq[plane, :ng, :], freq[plane, ng:, :]
                freq[plane, :ng, :] = real * mean + reflect_plane(real) * odd
                freq[plane, ng:, :] = imag * mean - reflect_plane(imag) * odd

            undo = table_dot(tables[2, 0], tables[2, 1], freq[plane])
            undo = jnp.concatenate([undo[:ng], undo[ng:]], axis=1)
            cells = dot_table(undo, tables[3, 0], tables[3, 1])
            cols = ng // gy_count
            for c in range(2):
                for y in range(gy_count):
                    for x in range(gz_count):
                        planes[y * gz_count + x, part, pl.ds(c * 4 + p, rows, stride=8), :] = cells[
                            x * rows : (x + 1) * rows, c * ng + y * cols : c * ng + (y + 1) * cols]
            return carry

        lax.fori_loop(0, 4, body, 0)

    own_home = [pltpu.make_async_copy(planes.at[slot, h], home_ref.at[slot, h], own_sem.at[h]) for h in range(PARTS)]

    def arrive(part):
        own_planes[part].wait()
        for step in order:
            fwd_copy(step, partner(step)[0], part).wait_recv()
        forward(part)

    def depart(part):
        backward(part)
        for step in order:
            back_copy(step, slot, part).start()
        own_home[part].start()

    for part in range(PARTS):
        own_green[part].wait()
        for step in order:
            green_copy(step, partner(step)[0], part).wait_recv()
        if part == 0:
            line_start(0)
    for part in range(PARTS):
        for step in order:
            fwd_copy(step, slot, part).start()
    for hop in range(1, reps):
        relay(hop, 0)
    line_start(1)
    for load in loads:
        load.wait()
    arrive(0)
    depart(0)
    relay(1, 1)
    arrive(1)
    for hop in range(2, reps):
        relay(hop, 1)
    depart(1)

    for part in range(PARTS):
        for step in order:
            green_copy(step, slot, part).wait_send()
            fwd_copy(step, slot, part).wait_send()
        for hop in range(reps):
            @pl.when((rep >= hop) & (rep + 1 < reps))
            def _():
                line_copy(rep - hop, part, right_send.at[hop], 1).wait_send()

            @pl.when((rep + hop < reps) & (rep >= 1))
            def _():
                line_copy(rep + hop, part, left_send.at[hop], -1).wait_send()
    for part in range(PARTS):
        own_home[part].wait()
        for step in order:
            back_copy(step, slot, part).wait_send()
            back_copy(step, partner(step)[0], part).wait_recv()


def fused_plan(charges, green):
    gy_count, gz_count, reps = lax.axis_size("gy"), lax.axis_size("gz"), lax.axis_size("rep")
    groups = gy_count * gz_count
    rows, cols, depth = charges.shape
    ng = rows * gz_count
    half = depth // 2
    each = half // groups
    step = 8
    forward_table, back_table = depth_tables(depth, groups, each)
    back_h, back_l = split_table(back_table / (ng * ng * depth))
    table_spec = pl.BlockSpec((depth, depth), lambda i: (0, 0))
    cells_spec = pl.BlockSpec((step, cols, depth), lambda i: (i, 0, 0))
    spec_spec = pl.BlockSpec((groups, PARTS, step * 8, cols), lambda i: (0, 0, i, 0))
    spec_shape = jax.ShapeDtypeStruct((groups, PARTS, rows * 8, cols), f32)
    limit = pltpu.CompilerParams(vmem_limit_bytes=63 * 2**20)

    k1, k2, _ = green.shape
    own_index = np.arange(half)
    opposite = np.where(own_index == 0, half, depth - own_index)
    quads = np.repeat(np.arange(half // 4), 8) * 4 + np.tile(np.arange(4), half // 2)
    pick = np.zeros((2 * depth, depth), np.float32)
    pick[np.arange(depth), own_index[quads]] = 1.0
    pick[depth + np.arange(depth), opposite[quads]] = 1.0
    index = np.arange(ng)
    halves = np.concatenate([index[0::2], index[1::2]])
    angle = 2.0 * np.pi * ((index[:, None] * index[None, :]) % ng) / ng
    cos, sin = np.cos(angle), np.sin(angle)
    waves = np.stack([cos, sin, -sin])
    waves = np.concatenate([waves, waves[:, :, halves], waves[:, halves, :]])
    waves = stacked_table(waves, 1)
    flips = np.stack([(rows_of[:, None] + rows_of[None, :]) % ng == 0 for rows_of in (index, halves)])
    flips = jnp.asarray(flips, bf16)

    dma = pltpu.SemaphoreType.DMA
    both = (groups, PARTS)
    home = pl.pallas_call(
        functools.partial(planes_kernel, gy_count, gz_count, reps),
        out_shape=spec_shape, name="planes",
        in_specs=[pl.BlockSpec(memory_space=pl.ANY)] * 6, out_specs=pl.BlockSpec(memory_space=pl.ANY),
        scratch_shapes=[
            pltpu.VMEM(charges.shape, f32),
            pltpu.VMEM((k1 * k2, depth), f32),
            pltpu.VMEM(pick.shape, bf16),
            pltpu.VMEM((2, depth, depth), bf16),
            pltpu.VMEM((groups, PARTS, k2 * 4, 2 * k1), f32),
            pltpu.VMEM(spec_shape.shape, f32),
            pltpu.VMEM(spec_shape.shape, f32),
            pltpu.VMEM((reps, PARTS, ng * each // PARTS, 2 * k1), f32),
            pltpu.VMEM((each, 2 * ng, ng), f32),
            pltpu.VMEM((4, 2, 2 * ng, 2 * ng), bf16),
            pltpu.VMEM((2, ng, ng), bf16),
            dma(both), dma(both), dma(both), dma(both), dma(both), dma(both),
            dma((reps, PARTS)), dma((reps, PARTS)), dma((reps, PARTS)), dma((2 * PARTS,)), dma((17,)), dma((4,)),
        ],
        compiler_params=pltpu.CompilerParams(
            collective_id=0, has_side_effects=True, vmem_limit_bytes=63 * 2**20),
    )(charges, green.reshape(k1 * k2, depth), jnp.asarray(pick, bf16), stacked_table(forward_table, 0), waves, flips)

    return pl.pallas_call(
        depth_out_kernel, grid=(rows // step,), out_shape=jax.ShapeDtypeStruct(charges.shape, f32), name="depth_out",
        in_specs=[table_spec, table_spec, spec_spec], out_specs=cells_spec, compiler_params=limit,
    )(back_h, back_l, home)


def on_device(charges, green):
    groups = lax.axis_size("gy") * lax.axis_size("gz")
    rows, cols, depth = charges.shape
    aligned = (
        cols % 128 == 0 and depth % 128 == 0 and depth == 16 * groups and rows % 8 == 0
        and green.shape[0] == 64 and lax.axis_size("rep") % 2 == 0 and lax.axis_size("rep") > 2
        and rows * lax.axis_size("gz") == cols * lax.axis_size("gy")
    )
    return fused_plan(charges, green) if aligned else slab_plan(charges, green)


def solution(mesh):
    placed = (P(("rep", "gz"), "gy", None), P("rep", ("gy", "gz"), None))
    return jax.shard_map(
        on_device,
        mesh=mesh,
        in_specs=placed,
        out_specs=P(("rep", "gz"), "gy", None),
        check_vma=False,
    )
```

profile of v0, /device:TPU:0, one launch (start us, length us, event | category | flops | bytes accessed | tf_op | source)
XLA Modules:
  0.0 120.0 jit_solution(15840115219583125158)
XLA Ops:
  0.0 112.1 %planes.1.spec_ref = f32[8,2,512,128]{3,2,1,0:T(8,128)} custom-call(f32[64,128,128]{2,1,0:T(8,128)} %cells_in.1, f32[2048,128]{1,0:T(8,128)} %bitcast.1, bf16[256,128]{1,0:T(8,128)(2,1)} %constant.16.clone.pick_in, bf16[2,128,128]{2,1,0:T(8,128)(2,1)} %constant.17.clone.depth_table, bf16[9,2,256,256]{3,2,1,0:T(8,128)(2,1)} %constant.14.clone.waves_ref, ...), custom_call_target="tpu_custom_call" | custom-call | tf_op jit(solution)/shard_map/planes/pallas_call | solution.py:487
  112.1 7.9 %depth_out.1 = f32[64,128,128]{2,1,0:T(8,128)} custom-call(bf16[128,128]{1,0:T(8,128)(2,1)} %constant.12.clone.high_ref, bf16[128,128]{1,0:T(8,128)(2,1)} %constant.13.clone.low_ref, f32[8,2,512,128]{3,2,1,0:T(8,128)} %planes.1.spec_ref), custom_call_target="tpu_custom_call" | custom-call | tf_op jit(solution)/shard_map/depth_out/pallas_call | solution.py:510
where the time goes:
time: 120 us
  Pallas kernels  120 us (100%)
    pallas_call x1, Pallas kernels, fused_plan(): pl.pallas_call(functools.partial(planes_kernel, gy_count, gz_count, reps)...  112 us
    pallas_call x1, Pallas kernels, fused_plan(): pl.pallas_call(depth_out_kernel, grid=(rows // step,), out_shape=jax.Shap...  7.92 us

commit v1 on v0

--- a/solution.py
+++ b/solution.py
@@ -110,6 +110,7 @@
 bf16 = jnp.bfloat16
 MESH = pl.DeviceIdType.MESH
 PARTS = 2
+HALVES = 2
 
 
 def split(values):
@@ -120,13 +121,6 @@
 def stacked_table(table, axis):
     rounded = table.astype(jnp.bfloat16)
     return jnp.asarray(np.stack([rounded, (table - rounded.astype(np.float64)).astype(jnp.bfloat16)], axis=axis))
-
-
-def split_table(table):
-    rounded = table.astype(jnp.bfloat16)
-    high = jnp.asarray(rounded)
-    low = jnp.asarray((table - rounded.astype(np.float64)).astype(jnp.bfloat16))
-    return high, low
 
 
 def dot(left, right, dims=((1,), (0,))):
@@ -161,13 +155,21 @@
     return np.stack(forward), np.stack(back)
 
 
+def wide_table(table, axis):
+    rounded = table.astype(jnp.bfloat16)
+    low = (table - rounded.astype(np.float64)).astype(jnp.bfloat16)
+    both = np.concatenate([rounded, rounded], axis=1 - axis)
+    return jnp.asarray(np.concatenate([both, np.concatenate([low, np.zeros_like(low)], axis=1 - axis)], axis=axis))
+
+
 def depth_in(table, cells, out):
     groups, parts, _, cols = out.shape
     rows, depth, step = cells.shape[0], cells.shape[2], 8
 
     def body(i, carry):
-        values = cells[pl.ds(i * step, step)].reshape(step * cols, depth)
-        result = table_dot(table[0], table[1], values, ((1,), (1,)))
+        values = jnp.concatenate(split(cells[pl.ds(i * step, step)].reshape(step * cols, depth)), axis=1)
+        both = dot(table[...], values, ((1,), (1,)))
+        result = both[:depth] + both[depth:]
         for row in range(step):
             piece = result[:, row * cols : (row + 1) * cols]
             at = pl.multiple_of(i * (step * 8) + row * 8, 8)
@@ -177,35 +179,61 @@
     lax.fori_loop(0, rows // step, body, 0)
 
 
-def depth_out_kernel(high_ref, low_ref, spec_ref, out_ref):
+def depth_out_kernel(table_ref, spec_ref, out_ref, held, sem):
     rows, cols, depth = out_ref.shape
-    pieces = [
-        spec_ref[:, :, row * 8 : (row + 1) * 8, :].reshape(high_ref.shape[0], cols) for row in range(rows)
-    ]
-    values = jnp.concatenate(pieces, axis=1)
-    result = dot_table(values, high_ref[...], low_ref[...], ((0,), (0,)))
-    out_ref[...] = result.reshape(rows, cols, depth)
-
-
-def pick_green(pick_ref, green_ref, out_ref):
-    groups, parts, _, _ = out_ref.shape
+    count = sem.shape[0]
+    step = rows // count
+
+    def copy(i):
+        at = pl.ds(i * step, step)
+        return pltpu.make_async_copy(held.at[at], out_ref.at[at], sem.at[i])
+
+    def body(i, carry):
+        pieces = [
+            spec_ref[:, :, pl.ds(pl.multiple_of((i * step + row) * 8, 8), 8), :].reshape(depth, cols) for row in range(step)
+        ]
+        values = jnp.concatenate(split(jnp.concatenate(pieces, axis=1)), axis=0)
+        both = dot(values, table_ref[...], ((0,), (0,)))
+        held[pl.ds(i * step, step)] = (both[:, :depth] + both[:, depth:]).reshape(step, cols, depth)
+        copy(i).start()
+        return carry
+
+    lax.fori_loop(0, count, body, 0)
+
+    def finish(i, carry):
+        copy(i).wait()
+        return carry
+
+    lax.fori_loop(0, count, finish, 0)
+
+
+def green_terms(green_ref):
     count = green_ref.shape[0] // 64
     rest = jnp.concatenate([green_ref[pl.ds(k2, 64, stride=count), :] for k2 in range(count)], axis=0)
-    result = None
+    terms = []
     for _ in range(3):
-        high = rest.astype(bf16)
-        rest = rest - high.astype(f32)
-        term = dot(pick_ref[...], high, ((1,), (1,)))
-        result = term if result is None else result + term
-    size = groups * parts * 8
+        terms.append(rest.astype(bf16))
+        rest = rest - terms[-1].astype(f32)
+    return jnp.concatenate(terms[:2], axis=1), terms[2]
+
+
+def pick_green(part, pick_ref, terms, out_ref):
+    groups, parts, halves, rows, _ = out_ref.shape
+    size = groups * halves * 8
+    pick = pick_ref[part * 2 * size : (part + 1) * 2 * size, :]
+    first, last = terms
+    result = dot(jnp.concatenate([pick, pick], axis=1), first, ((1,), (1,))) + dot(pick, last, ((1,), (1,)))
     first_lanes = lax.broadcasted_iota(jnp.int32, (size, 128), 1) < 64
-    first_rows = lax.rem(lax.broadcasted_iota(jnp.int32, (size, 128), 0), 8) < 4
-    for pair in range(count // 2):
-        own = result[:size, pair * 128 : (pair + 1) * 128]
-        mirror = result[size:, pair * 128 : (pair + 1) * 128]
-        even = jnp.where(first_lanes, own, pltpu.roll(mirror, 64, 1))
-        odd = jnp.where(first_lanes, pltpu.roll(own, 64, 1), mirror)
-        out_ref[:, :, pair * 8 : (pair + 1) * 8, :] = jnp.where(first_rows, even, odd).reshape(groups, parts, 8, 128)
+    place = lax.rem(lax.broadcasted_iota(jnp.int32, (size, 128), 0), 8) // 2
+    for tile in range(rows // 8):
+        spread = []
+        for pair in (2 * tile, 2 * tile + 1):
+            own = result[:size, pair * 128 : (pair + 1) * 128]
+            mirror = result[size:, pair * 128 : (pair + 1) * 128]
+            spread.append(jnp.where(first_lanes, own, pltpu.roll(mirror, 64, 1)))
+            spread.append(jnp.where(first_lanes, pltpu.roll(own, 64, 1), mirror))
+        packed = jnp.where(place < 2, jnp.where(place < 1, spread[0], spread[1]), jnp.where(place < 3, spread[2], spread[3]))
+        out_ref[:, part, :, tile * 8 : (tile + 1) * 8, :] = packed.reshape(groups, halves, 8, 128)
 
 
 def planes_kernel(
@@ -219,8 +247,9 @@
     rep, gy, gz = lax.axis_index("rep"), lax.axis_index("gy"), lax.axis_index("gz")
     slot = gy * gz_count + gz
     rows = spec_ref.shape[2] // 8
-    ng = flips_ref.shape[1]
-    piece = gains_ref.shape[2]
+    ng = flips_ref.shape[0]
+    piece = gains_ref.shape[3]
+    quarters = [(part, half) for part in range(PARTS) for half in range(HALVES)]
 
     def partner(step):
         there_y = lax.rem(gy + step // gz_count, gy_count)
@@ -239,11 +268,11 @@
         copy.start()
 
     loads = []
-    for table, (kind, swap) in enumerate(((1, False), (0, True), (0, False), (2, True))):
+    for table, swap in enumerate((False, True, False, True)):
         minus, plus = (1, 2) if swap else (2, 1)
         for quadrant, wave in enumerate((0, minus, plus, 0)):
             loads.append(pltpu.make_async_copy(
-                waves_ref.at[3 * kind + wave],
+                waves_ref.at[wave],
                 tables.at[table, :, pl.ds(quadrant // 2 * ng, ng), pl.ds(quadrant % 2 * ng, ng)],
                 table_sem.at[4 * table + quadrant]))
     loads.append(pltpu.make_async_copy(flips_ref, flips, table_sem.at[16]))
@@ -255,18 +284,27 @@
     barrier = pltpu.get_barrier_semaphore()
     for step in order:
         pl.semaphore_signal(barrier, inc=1, device_id=partner(step)[1], device_id_type=MESH)
-    for step in (1, -1):
-        pl.semaphore_signal(barrier, inc=1, device_id=along(step), device_id_type=MESH)
+
+    @pl.when(rep + 1 < reps)
+    def _():
+        pl.semaphore_signal(barrier, inc=1, device_id=along(1), device_id_type=MESH)
+
+    @pl.when(rep >= 1)
+    def _():
+        pl.semaphore_signal(barrier, inc=1, device_id=along(-1), device_id_type=MESH)
+
     for copy in inputs[:2]:
         copy.wait()
-    pick_green(pick_ref, field_ref, gains_ref)
-    pl.semaphore_wait(barrier, groups + 1)
-
-    def green_copy(step, source, part):
+    terms = green_terms(field_ref)
+    pick_green(0, pick_ref, terms, gains_ref)
+    pl.semaphore_wait(barrier, groups - 1 + lax.div(rep + reps - 1, reps) + lax.div(2 * reps - 2 - rep, reps))
+
+    def green_copy(step, source, part, half):
         there, device = partner(step)
         return pltpu.make_async_remote_copy(
-            src_ref=gains_ref.at[there, part], dst_ref=green.at[rep, part, pl.ds(source * piece, piece), :],
-            send_sem=green_send.at[there, part], recv_sem=green_recv.at[source, part], device_id=device, device_id_type=MESH)
+            src_ref=gains_ref.at[there, part, half], dst_ref=green.at[rep, part, half, pl.ds(source * piece, piece), :],
+            send_sem=green_send.at[there, part, half], recv_sem=green_recv.at[source, part, half],
+            device_id=device, device_id_type=MESH)
 
     def fwd_copy(step, source, part):
         there, device = partner(step)
@@ -280,53 +318,77 @@
             src_ref=planes.at[there, part], dst_ref=home_ref.at[source, part],
             send_sem=back_send.at[there, part], recv_sem=back_recv.at[source, part], device_id=device, device_id_type=MESH)
 
-    def line_copy(block, part, sem, step):
+    def line_copy(block, at, sem, step):
         return pltpu.make_async_remote_copy(
-            src_ref=green.at[block, part], dst_ref=green.at[block, part], send_sem=sem.at[part],
-            recv_sem=line_recv.at[block, part], device_id=along(step), device_id_type=MESH)
-
-    own_green = [
-        pltpu.make_async_copy(
-            gains_ref.at[slot, h], green.at[rep, h, pl.ds(slot * piece, piece), :], own_sem.at[PARTS + h])
-        for h in range(PARTS)
-    ]
+            src_ref=green.at[(block, *at)], dst_ref=green.at[(block, *at)], send_sem=sem.at[at],
+            recv_sem=line_recv.at[(block, *at)], device_id=along(step), device_id_type=MESH)
+
+    own_green = {
+        (part, half): pltpu.make_async_copy(
+            gains_ref.at[slot, part, half], green.at[rep, part, half, pl.ds(slot * piece, piece), :],
+            own_sem.at[PARTS + part * HALVES + half])
+        for part, half in quarters
+    }
     own_planes = [pltpu.make_async_copy(spec_ref.at[slot, h], planes.at[slot, h], own_sem.at[h]) for h in range(PARTS)]
-    for part in range(PARTS):
-        for step in order:
-            green_copy(step, slot, part).start()
-    for copy in own_green:
-        copy.start()
+
+    def green_start(part):
+        for half in range(HALVES):
+            for step in order:
+                green_copy(step, slot, part, half).start()
+
+    green_start(0)
+    for part in range(1, PARTS):
+        pick_green(part, pick_ref, terms, gains_ref)
+        green_start(part)
+    for at in quarters:
+        own_green[at].start()
     for copy in inputs[2:]:
         copy.wait()
     depth_in(depth_ref, cells_ref, spec_ref)
+    for part in range(PARTS):
+        for step in order:
+            fwd_copy(step, slot, part).start()
     for copy in own_planes:
         copy.start()
 
-    def line_start(part):
-        @pl.when(rep + 1 < reps)
+    def green_wait(at):
+        own_green[at].wait()
+        for step in order:
+            green_copy(step, partner(step)[0], *at).wait_recv()
+
+    def line_start(at, hop=None):
+        right, left = rep + 1 < reps, rep >= 1
+        if hop is not None:
+            right, left = right & (rep == hop), left & (rep + hop == reps - 1)
+
+        @pl.when(right)
         def _():
-            line_copy(rep, part, right_send.at[0], 1).start()
-
-        @pl.when(rep >= 1)
+            line_copy(rep, at, right_send.at[0], 1).start()
+
+        @pl.when(left)
         def _():
-            line_copy(rep, part, left_send.at[0], -1).start()
-
-    def relay(hop, part):
-        @pl.when(rep >= hop)
-        def _():
-            line_copy(rep - hop, part, right_send.at[hop], 1).wait_recv()
-
+            line_copy(rep, at, left_send.at[0], -1).start()
+
+    def relay(hop, at):
         @pl.when((rep >= hop) & (rep + 1 < reps))
         def _():
-            line_copy(rep - hop, part, right_send.at[hop], 1).start()
-
-        @pl.when(rep + hop < reps)
-        def _():
-            line_copy(rep + hop, part, left_send.at[hop], -1).wait_recv()
+            line_copy(rep - hop, at, right_send.at[hop], 1).wait_recv()
+            line_copy(rep - hop, at, right_send.at[hop], 1).start()
 
         @pl.when((rep + hop < reps) & (rep >= 1))
         def _():
-            line_copy(rep + hop, part, left_send.at[hop], -1).start()
+            line_copy(rep + hop, at, left_send.at[hop], -1).wait_recv()
+            line_copy(rep + hop, at, left_send.at[hop], -1).start()
+
+    def line_end(at):
+        for hop in range(1, reps):
+            @pl.when(rep + 1 == reps)
+            def _():
+                line_copy(rep - hop, at, right_send.at[hop], 1).wait_recv()
+
+            @pl.when(rep == 0)
+            def _():
+                line_copy(rep + hop, at, left_send.at[hop], -1).wait_recv()
 
     def load_plane(part, row):
         bands = []
@@ -347,20 +409,18 @@
 
     def reflect_plane(values):
         high, low = split(values)
-        turned = dot(flips[0], high) + dot(flips[0], low)
+        turned = dot(flips[...], high) + dot(flips[...], low)
         high, low = split(turned)
-        return dot(high, flips[1]) + dot(low, flips[1])
-
-    def backward(part):
+        return dot(high, flips[...]) + dot(low, flips[...])
+
+    def backward(part, half):
         def body(p, carry):
-            plane = part * 4 + p
+            row = half * 2 + p
+            plane = part * 4 + row
             own, mirror = [], []
             lane = lax.broadcasted_iota(jnp.int32, (ng, 128), 1)
             for r in range(0, reps, 2):
-                one, two = (
-                    jnp.concatenate([green[q, part, pl.ds(4 * odd + p, ng // 2, stride=8), :] for odd in range(2)], axis=0)
-                    for q in (r, r + 1)
-                )
+                one, two = (green[q, part, half, pl.ds(p, ng, stride=2), :] for q in (r, r + 1))
                 own.append(jnp.where(lane < 64, one, pltpu.roll(two, 64, 1)))
                 mirror.append(jnp.where(lane < 64, pltpu.roll(one, 64, 1), two))
             own = jnp.concatenate(own, axis=1).T
@@ -388,11 +448,11 @@
             for c in range(2):
                 for y in range(gy_count):
                     for x in range(gz_count):
-                        planes[y * gz_count + x, part, pl.ds(c * 4 + p, rows, stride=8), :] = cells[
+                        planes[y * gz_count + x, part, pl.ds(c * 4 + row, rows, stride=8), :] = cells[
                             x * rows : (x + 1) * rows, c * ng + y * cols : c * ng + (y + 1) * cols]
             return carry
 
-        lax.fori_loop(0, 4, body, 0)
+        lax.fori_loop(0, 2, body, 0)
 
     own_home = [pltpu.make_async_copy(planes.at[slot, h], home_ref.at[slot, h], own_sem.at[h]) for h in range(PARTS)]
 
@@ -403,45 +463,60 @@
         forward(part)
 
     def depart(part):
-        backward(part)
         for step in order:
             back_copy(step, slot, part).start()
         own_home[part].start()
 
-    for part in range(PARTS):
-        own_green[part].wait()
-        for step in order:
-            green_copy(step, partner(step)[0], part).wait_recv()
-        if part == 0:
-            line_start(0)
+    first, second = quarters[:HALVES], quarters[HALVES:]
+
+    def second_start(hop):
+        for at in second:
+            line_start(at, hop)
+
+    for at in first:
+        green_wait(at)
+        line_start(at)
+    relay(1, first[0])
+    for at in second:
+        green_wait(at)
+    second_start(0)
+    relay(1, first[1])
+    second_start(1)
+    for hop in range(2, reps - 1):
+        for at in first:
+            relay(hop, at)
+        second_start(hop)
+    for load in loads:
+        load.wait()
+    relay(1, second[0])
+    arrive(0)
+    relay(1, second[1])
+    for at in first:
+        line_end(at)
+        for hop in range(2, reps - 1):
+            relay(hop, second[at[1]])
+        backward(*at)
+    depart(0)
+    arrive(1)
+    for at in second:
+        line_end(at)
+        backward(*at)
+    depart(1)
+
     for part in range(PARTS):
         for step in order:
-            fwd_copy(step, slot, part).start()
-    for hop in range(1, reps):
-        relay(hop, 0)
-    line_start(1)
-    for load in loads:
-        load.wait()
-    arrive(0)
-    depart(0)
-    relay(1, 1)
-    arrive(1)
-    for hop in range(2, reps):
-        relay(hop, 1)
-    depart(1)
-
-    for part in range(PARTS):
+            fwd_copy(step, slot, part).wait_send()
+    for at in quarters:
         for step in order:
-            green_copy(step, slot, part).wait_send()
-            fwd_copy(step, slot, part).wait_send()
+            green_copy(step, slot, *at).wait_send()
         for hop in range(reps):
             @pl.when((rep >= hop) & (rep + 1 < reps))
             def _():
-                line_copy(rep - hop, part, right_send.at[hop], 1).wait_send()
+                line_copy(rep - hop, at, right_send.at[hop], 1).wait_send()
 
             @pl.when((rep + hop < reps) & (rep >= 1))
             def _():
-                line_copy(rep + hop, part, left_send.at[hop], -1).wait_send()
+                line_copy(rep + hop, at, left_send.at[hop], -1).wait_send()
     for part in range(PARTS):
         own_home[part].wait()
         for step in order:
@@ -456,34 +531,28 @@
     ng = rows * gz_count
     half = depth // 2
     each = half // groups
-    step = 8
     forward_table, back_table = depth_tables(depth, groups, each)
-    back_h, back_l = split_table(back_table / (ng * ng * depth))
-    table_spec = pl.BlockSpec((depth, depth), lambda i: (0, 0))
-    cells_spec = pl.BlockSpec((step, cols, depth), lambda i: (i, 0, 0))
-    spec_spec = pl.BlockSpec((groups, PARTS, step * 8, cols), lambda i: (0, 0, i, 0))
+    chunks = rows // 16
     spec_shape = jax.ShapeDtypeStruct((groups, PARTS, rows * 8, cols), f32)
-    limit = pltpu.CompilerParams(vmem_limit_bytes=63 * 2**20)
 
     k1, k2, _ = green.shape
     own_index = np.arange(half)
     opposite = np.where(own_index == 0, half, depth - own_index)
-    quads = np.repeat(np.arange(half // 4), 8) * 4 + np.tile(np.arange(4), half // 2)
-    pick = np.zeros((2 * depth, depth), np.float32)
-    pick[np.arange(depth), own_index[quads]] = 1.0
-    pick[depth + np.arange(depth), opposite[quads]] = 1.0
+    quad, place = np.divmod(np.arange(groups * HALVES * 8), 8)
+    quad = quad // HALVES * PARTS * HALVES + quad % HALVES
+    pick = []
+    for part in range(PARTS):
+        bins = (quad + part * HALVES) * 2 + place % 2
+        pick += [own_index[bins], opposite[bins]]
+    pick = (np.concatenate(pick)[:, None] == np.arange(depth)[None, :]).astype(np.float32)
     index = np.arange(ng)
-    halves = np.concatenate([index[0::2], index[1::2]])
     angle = 2.0 * np.pi * ((index[:, None] * index[None, :]) % ng) / ng
     cos, sin = np.cos(angle), np.sin(angle)
-    waves = np.stack([cos, sin, -sin])
-    waves = np.concatenate([waves, waves[:, :, halves], waves[:, halves, :]])
-    waves = stacked_table(waves, 1)
-    flips = np.stack([(rows_of[:, None] + rows_of[None, :]) % ng == 0 for rows_of in (index, halves)])
-    flips = jnp.asarray(flips, bf16)
+    waves = stacked_table(np.stack([cos, sin, -sin]), 1)
+    flips = jnp.asarray((index[:, None] + index[None, :]) % ng == 0, bf16)
 
     dma = pltpu.SemaphoreType.DMA
-    both = (groups, PARTS)
+    both, lines = (groups, PARTS), (reps, PARTS, HALVES)
     home = pl.pallas_call(
         functools.partial(planes_kernel, gy_count, gz_count, reps),
         out_shape=spec_shape, name="planes",
@@ -492,25 +561,32 @@
             pltpu.VMEM(charges.shape, f32),
             pltpu.VMEM((k1 * k2, depth), f32),
             pltpu.VMEM(pick.shape, bf16),
-            pltpu.VMEM((2, depth, depth), bf16),
-            pltpu.VMEM((groups, PARTS, k2 * 4, 2 * k1), f32),
+            pltpu.VMEM((2 * depth, 2 * depth), bf16),
+            pltpu.VMEM((groups, PARTS, HALVES, k2 * 2, 2 * k1), f32),
             pltpu.VMEM(spec_shape.shape, f32),
             pltpu.VMEM(spec_shape.shape, f32),
-            pltpu.VMEM((reps, PARTS, ng * each // PARTS, 2 * k1), f32),
+            pltpu.VMEM((reps, PARTS, HALVES, ng * 2, 2 * k1), f32),
             pltpu.VMEM((each, 2 * ng, ng), f32),
             pltpu.VMEM((4, 2, 2 * ng, 2 * ng), bf16),
-            pltpu.VMEM((2, ng, ng), bf16),
-            dma(both), dma(both), dma(both), dma(both), dma(both), dma(both),
-            dma((reps, PARTS)), dma((reps, PARTS)), dma((reps, PARTS)), dma((2 * PARTS,)), dma((17,)), dma((4,)),
+            pltpu.VMEM((ng, ng), bf16),
+            dma(both), dma(both), dma(both), dma(both), dma((*both, HALVES)), dma((*both, HALVES)),
+            dma(lines), dma(lines), dma(lines), dma((PARTS * (1 + HALVES),)), dma((17,)), dma((4,)),
         ],
         compiler_params=pltpu.CompilerParams(
-            collective_id=0, has_side_effects=True, vmem_limit_bytes=63 * 2**20),
-    )(charges, green.reshape(k1 * k2, depth), jnp.asarray(pick, bf16), stacked_table(forward_table, 0), waves, flips)
-
+            collective_id=0, has_side_effects=True, vmem_limit_bytes=44 * 2**20),
+    )(*(
+        pltpu.with_memory_space_constraint(value, pltpu.HBM)
+        for value in (
+            charges, green.reshape(k1 * k2, depth), jnp.asarray(pick, bf16), wide_table(forward_table, 0), waves, flips)
+    ))
+
+    vmem = pl.BlockSpec(memory_space=pltpu.VMEM)
     return pl.pallas_call(
-        depth_out_kernel, grid=(rows // step,), out_shape=jax.ShapeDtypeStruct(charges.shape, f32), name="depth_out",
-        in_specs=[table_spec, table_spec, spec_spec], out_specs=cells_spec, compiler_params=limit,
-    )(back_h, back_l, home)
+        depth_out_kernel, out_shape=jax.ShapeDtypeStruct(charges.shape, f32), name="depth_out",
+        in_specs=[vmem, vmem], out_specs=pl.BlockSpec(memory_space=pl.ANY),
+        scratch_shapes=[pltpu.VMEM(charges.shape, f32), dma((chunks,))],
+        compiler_params=pltpu.CompilerParams(vmem_limit_bytes=16 * 2**20),
+    )(wide_table(back_table / (ng * ng * depth), 1), home)
 
 
 def on_device(charges, green):

time: 120 us -> 114 us (0.950)
  Pallas kernels: 120 us -> 114 us
    pallas_call x1, Pallas kernels: 7.92 us -> 2.95 us  [fused_plan(): pl.pallas_call(depth_out_kernel, out_shape=jax.ShapeDtypeStruct(charges.s...]
    pallas_call x1, Pallas kernels: 112 us -> 111 us  [fused_plan(): pl.pallas_call(functools.partial(planes_kernel, gy_count, gz_count, reps)...]
where the time goes in v1:
time: 114 us
  Pallas kernels  114 us (100%)
    pallas_call x1, Pallas kernels, fused_plan(): pl.pallas_call(functools.partial(planes_kernel, gy_count, gz_count, reps)...  111 us
    pallas_call x1, Pallas kernels, fused_plan(): pl.pallas_call(depth_out_kernel, out_shape=jax.ShapeDtypeStruct(charges.s...  2.95 us

profile of v1, /device:TPU:0, one launch (start us, length us, event | category | flops | bytes accessed | tf_op | source)
XLA Modules:
  0.0 113.8 jit_solution(9652320818371139663)
XLA Ops:
  0.0 0.0 copy-start
  0.0 110.6 %planes.1.spec_ref = f32[8,2,512,128]{3,2,1,0:T(8,128)S(1)} custom-call(f32[64,128,128]{2,1,0:T(8,128)} %cells_in.1, f32[2048,128]{1,0:T(8,128)} %bitcast.1, bf16[512,128]{1,0:T(8,128)(2,1)} %constant.12.clone.pick_in, bf16[256,256]{1,0:T(8,128)(2,1)} %constant.13.clone.depth_table, bf16[3,2,256,256]{3,2,1,0:T(8,128)(2,1)} %constant.10.clone.waves_ref, ...), custom_call_target="tpu_custom_call" | custom-call | tf_op jit(solution)/shard_map/planes/pallas_call | solution.py:556
  110.6 0.0 copy-done
  110.7 3.0 %depth_out.1 = f32[64,128,128]{2,1,0:T(8,128)} custom-call(bf16[256,256]{1,0:T(8,128)(2,1)S(1)} %copy-done, f32[8,2,512,128]{3,2,1,0:T(8,128)S(1)} %planes.1.spec_ref), custom_call_target="tpu_custom_call" | custom-call | tf_op jit(solution)/shard_map/depth_out/pallas_call | solution.py:584
Async XLA Ops:
  0.0 110.6 %copy-start = (bf16[256,256]{1,0:T(8,128)(2,1)S(1)}, bf16[256,256]{1,0:T(8,128)(2,1)}, u32[]{:S(2)}) copy-start(bf16[256,256]{1,0:T(8,128)(2,1)} %constant.14.clone.table_ref) | copy-start | bytes 393220

commit v2 on v1

--- a/solution.py
+++ b/solution.py
@@ -207,9 +207,10 @@
     lax.fori_loop(0, count, finish, 0)
 
 
-def green_terms(green_ref):
-    count = green_ref.shape[0] // 64
-    rest = jnp.concatenate([green_ref[pl.ds(k2, 64, stride=count), :] for k2 in range(count)], axis=0)
+def green_terms(count, green_ref):
+    size, pitch, lanes = green_ref.shape
+    flat = green_ref.reshape(size * pitch, lanes)
+    rest = jnp.concatenate([flat[pl.ds(k2, size, stride=pitch), :] for k2 in range(count)], axis=0)
     terms = []
     for _ in range(3):
         terms.append(rest.astype(bf16))
@@ -262,22 +263,20 @@
     inputs = [
         pltpu.make_async_copy(source, held, in_sem.at[i])
         for i, (source, held) in enumerate((
-            (green_in, field_ref), (pick_in, pick_ref), (cells_in, cells_ref), (depth_table, depth_ref)))
+            (green_in, field_ref.at[:, pl.ds(0, green_in.shape[1]), :]), (pick_in, pick_ref), (cells_in, cells_ref), (depth_table, depth_ref)))
     ]
-    for copy in inputs:
+    for copy in inputs[:2]:
         copy.start()
 
     loads = []
-    for table, swap in enumerate((False, True, False, True)):
+    for table, swap in enumerate((False, True)):
         minus, plus = (1, 2) if swap else (2, 1)
         for quadrant, wave in enumerate((0, minus, plus, 0)):
             loads.append(pltpu.make_async_copy(
                 waves_ref.at[wave],
                 tables.at[table, :, pl.ds(quadrant // 2 * ng, ng), pl.ds(quadrant % 2 * ng, ng)],
                 table_sem.at[4 * table + quadrant]))
-    loads.append(pltpu.make_async_copy(flips_ref, flips, table_sem.at[16]))
-    for load in loads:
-        load.start()
+    loads.append(pltpu.make_async_copy(flips_ref, flips, table_sem.at[8]))
 
     order = sorted(range(1, groups), key=lambda s: (-(s % gz_count), s))
 
@@ -295,7 +294,9 @@
 
     for copy in inputs[:2]:
         copy.wait()
-    terms = green_terms(field_ref)
+    for copy in inputs[2:]:
+        copy.start()
+    terms = green_terms(green_in.shape[1], field_ref)
     pick_green(0, pick_ref, terms, gains_ref)
     pl.semaphore_wait(barrier, groups - 1 + lax.div(rep + reps - 1, reps) + lax.div(2 * reps - 2 - rep, reps))
 
@@ -303,33 +304,29 @@
         there, device = partner(step)
         return pltpu.make_async_remote_copy(
             src_ref=gains_ref.at[there, part, half], dst_ref=green.at[rep, part, half, pl.ds(source * piece, piece), :],
-            send_sem=green_send.at[there, part, half], recv_sem=green_recv.at[source, part, half],
+            send_sem=green_send.at[0], recv_sem=green_recv.at[part, half],
             device_id=device, device_id_type=MESH)
 
     def fwd_copy(step, source, part):
         there, device = partner(step)
         return pltpu.make_async_remote_copy(
             src_ref=spec_ref.at[there, part], dst_ref=planes.at[source, part],
-            send_sem=fwd_send.at[there, part], recv_sem=fwd_recv.at[source, part], device_id=device, device_id_type=MESH)
+            send_sem=fwd_send.at[0], recv_sem=fwd_recv.at[part], device_id=device, device_id_type=MESH)
 
     def back_copy(step, source, part):
         there, device = partner(step)
         return pltpu.make_async_remote_copy(
             src_ref=planes.at[there, part], dst_ref=home_ref.at[source, part],
-            send_sem=back_send.at[there, part], recv_sem=back_recv.at[source, part], device_id=device, device_id_type=MESH)
+            send_sem=back_send.at[0], recv_sem=back_recv.at[0], device_id=device, device_id_type=MESH)
+
+    def whole(ref, sem):
+        return pltpu.make_async_remote_copy(
+            src_ref=ref, dst_ref=ref, send_sem=sem, recv_sem=sem, device_id=partner(1)[1], device_id_type=MESH)
 
     def line_copy(block, at, sem, step):
         return pltpu.make_async_remote_copy(
-            src_ref=green.at[(block, *at)], dst_ref=green.at[(block, *at)], send_sem=sem.at[at],
+            src_ref=green.at[(block, *at)], dst_ref=green.at[(block, *at)], send_sem=sem,
             recv_sem=line_recv.at[(block, *at)], device_id=along(step), device_id_type=MESH)
-
-    own_green = {
-        (part, half): pltpu.make_async_copy(
-            gains_ref.at[slot, part, half], green.at[rep, part, half, pl.ds(slot * piece, piece), :],
-            own_sem.at[PARTS + part * HALVES + half])
-        for part, half in quarters
-    }
-    own_planes = [pltpu.make_async_copy(spec_ref.at[slot, h], planes.at[slot, h], own_sem.at[h]) for h in range(PARTS)]
 
     def green_start(part):
         for half in range(HALVES):
@@ -340,21 +337,21 @@
     for part in range(1, PARTS):
         pick_green(part, pick_ref, terms, gains_ref)
         green_start(part)
-    for at in quarters:
-        own_green[at].start()
+    for part, half in quarters:
+        green[rep, part, half, pl.ds(slot * piece, piece), :] = gains_ref[slot, part, half]
     for copy in inputs[2:]:
         copy.wait()
+    for load in loads:
+        load.start()
     depth_in(depth_ref, cells_ref, spec_ref)
     for part in range(PARTS):
         for step in order:
             fwd_copy(step, slot, part).start()
-    for copy in own_planes:
-        copy.start()
+    planes[slot] = spec_ref[slot]
+    others = pl.ds(0, groups - 1)
 
     def green_wait(at):
-        own_green[at].wait()
-        for step in order:
-            green_copy(step, partner(step)[0], *at).wait_recv()
+        whole(green.at[(rep, *at, pl.ds(0, (groups - 1) * piece))], green_recv.at[at]).wait_recv()
 
     def line_start(at, hop=None):
         right, left = rep + 1 < reps, rep >= 1
@@ -441,9 +438,9 @@
                 freq[plane, :ng, :] = real * mean + reflect_plane(real) * odd
                 freq[plane, ng:, :] = imag * mean - reflect_plane(imag) * odd
 
-            undo = table_dot(tables[2, 0], tables[2, 1], freq[plane])
+            undo = table_dot(tables[0, 0], tables[0, 1], freq[plane])
             undo = jnp.concatenate([undo[:ng], undo[ng:]], axis=1)
-            cells = dot_table(undo, tables[3, 0], tables[3, 1])
+            cells = dot_table(undo, tables[1, 0], tables[1, 1])
             cols = ng // gy_count
             for c in range(2):
                 for y in range(gy_count):
@@ -457,9 +454,7 @@
     own_home = [pltpu.make_async_copy(planes.at[slot, h], home_ref.at[slot, h], own_sem.at[h]) for h in range(PARTS)]
 
     def arrive(part):
-        own_planes[part].wait()
-        for step in order:
-            fwd_copy(step, partner(step)[0], part).wait_recv()
+        whole(planes.at[others, part], fwd_recv.at[part]).wait_recv()
         forward(part)
 
     def depart(part):
@@ -493,35 +488,31 @@
     relay(1, second[1])
     for at in first:
         line_end(at)
+        backward(*at)
+        if at == first[-1]:
+            depart(0)
         for hop in range(2, reps - 1):
             relay(hop, second[at[1]])
-        backward(*at)
-    depart(0)
     arrive(1)
     for at in second:
         line_end(at)
         backward(*at)
     depart(1)
 
-    for part in range(PARTS):
-        for step in order:
-            fwd_copy(step, slot, part).wait_send()
-    for at in quarters:
-        for step in order:
-            green_copy(step, slot, *at).wait_send()
-        for hop in range(reps):
-            @pl.when((rep >= hop) & (rep + 1 < reps))
-            def _():
-                line_copy(rep - hop, at, right_send.at[hop], 1).wait_send()
-
-            @pl.when((rep + hop < reps) & (rep >= 1))
-            def _():
-                line_copy(rep + hop, at, left_send.at[hop], -1).wait_send()
+    whole(gains_ref.at[others], green_send.at[0]).wait_send()
+    whole(spec_ref.at[others], fwd_send.at[0]).wait_send()
+    for hop in range(reps):
+        @pl.when((rep >= hop) & (rep + 1 < reps))
+        def _():
+            whole(green.at[rep - hop], right_send.at[hop]).wait_send()
+
+        @pl.when((rep + hop < reps) & (rep >= 1))
+        def _():
+            whole(green.at[rep + hop], left_send.at[hop]).wait_send()
     for part in range(PARTS):
         own_home[part].wait()
-        for step in order:
-            back_copy(step, slot, part).wait_send()
-            back_copy(step, partner(step)[0], part).wait_recv()
+    whole(planes.at[others], back_send.at[0]).wait_send()
+    whole(home_ref.at[others], back_recv.at[0]).wait_recv()
 
 
 def fused_plan(charges, green):
@@ -552,14 +543,13 @@
     flips = jnp.asarray((index[:, None] + index[None, :]) % ng == 0, bf16)
 
     dma = pltpu.SemaphoreType.DMA
-    both, lines = (groups, PARTS), (reps, PARTS, HALVES)
     home = pl.pallas_call(
         functools.partial(planes_kernel, gy_count, gz_count, reps),
         out_shape=spec_shape, name="planes",
         in_specs=[pl.BlockSpec(memory_space=pl.ANY)] * 6, out_specs=pl.BlockSpec(memory_space=pl.ANY),
         scratch_shapes=[
             pltpu.VMEM(charges.shape, f32),
-            pltpu.VMEM((k1 * k2, depth), f32),
+            pltpu.VMEM((k1, k2 + 8, depth), f32),
             pltpu.VMEM(pick.shape, bf16),
             pltpu.VMEM((2 * depth, 2 * depth), bf16),
             pltpu.VMEM((groups, PARTS, HALVES, k2 * 2, 2 * k1), f32),
@@ -567,17 +557,17 @@
             pltpu.VMEM(spec_shape.shape, f32),
             pltpu.VMEM((reps, PARTS, HALVES, ng * 2, 2 * k1), f32),
             pltpu.VMEM((each, 2 * ng, ng), f32),
-            pltpu.VMEM((4, 2, 2 * ng, 2 * ng), bf16),
+            pltpu.VMEM((2, 2, 2 * ng, 2 * ng), bf16),
             pltpu.VMEM((ng, ng), bf16),
-            dma(both), dma(both), dma(both), dma(both), dma((*both, HALVES)), dma((*both, HALVES)),
-            dma(lines), dma(lines), dma(lines), dma((PARTS * (1 + HALVES),)), dma((17,)), dma((4,)),
+            dma((1,)), dma((PARTS,)), dma((1,)), dma((1,)), dma((1,)), dma((PARTS, HALVES)),
+            dma((reps,)), dma((reps,)), dma((reps, PARTS, HALVES)), dma((PARTS,)), dma((9,)), dma((4,)),
         ],
         compiler_params=pltpu.CompilerParams(
             collective_id=0, has_side_effects=True, vmem_limit_bytes=44 * 2**20),
     )(*(
         pltpu.with_memory_space_constraint(value, pltpu.HBM)
         for value in (
-            charges, green.reshape(k1 * k2, depth), jnp.asarray(pick, bf16), wide_table(forward_table, 0), waves, flips)
+            charges, green, jnp.asarray(pick, bf16), wide_table(forward_table, 0), waves, flips)
     ))
 
     vmem = pl.BlockSpec(memory_space=pltpu.VMEM)

time: 114 us -> 112 us (0.982)
  Pallas kernels: 114 us -> 112 us
    pallas_call x1, Pallas kernels: 111 us -> 109 us  [fused_plan(): pl.pallas_call(functools.partial(planes_kernel, gy_count, gz_count, reps)...]
where the time goes in v2:
time: 112 us
  Pallas kernels  112 us (100%)
    pallas_call x1, Pallas kernels, fused_plan(): pl.pallas_call(functools.partial(planes_kernel, gy_count, gz_count, reps)...  109 us
    pallas_call x1, Pallas kernels, fused_plan(): pl.pallas_call(depth_out_kernel, out_shape=jax.ShapeDtypeStruct(charges.s...  2.96 us

profile of v2, /device:TPU:0, one launch (start us, length us, event | category | flops | bytes accessed | tf_op | source)
XLA Modules:
  0.0 111.8 jit_solution(5278343189440547231)
XLA Ops:
  0.0 0.0 copy-start
  0.0 108.8 %planes.1.spec_ref = f32[8,2,512,128]{3,2,1,0:T(8,128)S(1)} custom-call(f32[64,128,128]{2,1,0:T(8,128)} %cells_in.1, f32[64,32,128]{2,1,0:T(8,128)} %green_in.1, bf16[512,128]{1,0:T(8,128)(2,1)} %constant.12.clone.pick_in, bf16[256,256]{1,0:T(8,128)(2,1)} %constant.13.clone.depth_table, bf16[3,2,256,256]{3,2,1,0:T(8,128)(2,1)} %constant.10.clone.waves_ref, ...), custom_call_target="tpu_custom_call" | custom-call | tf_op jit(solution)/shard_map/planes/pallas_call | solution.py:546
  108.8 0.0 copy-done
  108.8 3.0 %depth_out.1 = f32[64,128,128]{2,1,0:T(8,128)} custom-call(bf16[256,256]{1,0:T(8,128)(2,1)S(1)} %copy-done, f32[8,2,512,128]{3,2,1,0:T(8,128)S(1)} %planes.1.spec_ref), custom_call_target="tpu_custom_call" | custom-call | tf_op jit(solution)/shard_map/depth_out/pallas_call | solution.py:574
Async XLA Ops:
  0.0 108.8 %copy-start = (bf16[256,256]{1,0:T(8,128)(2,1)S(1)}, bf16[256,256]{1,0:T(8,128)(2,1)}, u32[]{:S(2)}) copy-start(bf16[256,256]{1,0:T(8,128)(2,1)} %constant.14.clone.table_ref) | copy-start | bytes 393220

commit v3 on v2

--- a/solution.py
+++ b/solution.py
@@ -181,49 +181,32 @@
 
 def depth_out_kernel(table_ref, spec_ref, out_ref, held, sem):
     rows, cols, depth = out_ref.shape
-    count = sem.shape[0]
-    step = rows // count
-
-    def copy(i):
-        at = pl.ds(i * step, step)
-        return pltpu.make_async_copy(held.at[at], out_ref.at[at], sem.at[i])
-
-    def body(i, carry):
-        pieces = [
-            spec_ref[:, :, pl.ds(pl.multiple_of((i * step + row) * 8, 8), 8), :].reshape(depth, cols) for row in range(step)
-        ]
+    step = rows // sem.shape[0]
+    copies = []
+    for start in range(0, rows, step):
+        pieces = [spec_ref[:, :, row * 8 : (row + 1) * 8, :].reshape(depth, cols) for row in range(start, start + step)]
         values = jnp.concatenate(split(jnp.concatenate(pieces, axis=1)), axis=0)
         both = dot(values, table_ref[...], ((0,), (0,)))
-        held[pl.ds(i * step, step)] = (both[:, :depth] + both[:, depth:]).reshape(step, cols, depth)
-        copy(i).start()
-        return carry
-
-    lax.fori_loop(0, count, body, 0)
-
-    def finish(i, carry):
-        copy(i).wait()
-        return carry
-
-    lax.fori_loop(0, count, finish, 0)
+        at = pl.ds(start, step)
+        held[at] = (both[:, :depth] + both[:, depth:]).reshape(step, cols, depth)
+        copies.append(pltpu.make_async_copy(held.at[at], out_ref.at[at], sem.at[start // step]))
+        copies[-1].start()
+    for copy in copies:
+        copy.wait()
 
 
 def green_terms(count, green_ref):
     size, pitch, lanes = green_ref.shape
     flat = green_ref.reshape(size * pitch, lanes)
     rest = jnp.concatenate([flat[pl.ds(k2, size, stride=pitch), :] for k2 in range(count)], axis=0)
-    terms = []
-    for _ in range(3):
-        terms.append(rest.astype(bf16))
-        rest = rest - terms[-1].astype(f32)
-    return jnp.concatenate(terms[:2], axis=1), terms[2]
+    return jnp.concatenate(split(rest), axis=1)
 
 
 def pick_green(part, pick_ref, terms, out_ref):
     groups, parts, halves, rows, _ = out_ref.shape
     size = groups * halves * 8
     pick = pick_ref[part * 2 * size : (part + 1) * 2 * size, :]
-    first, last = terms
-    result = dot(jnp.concatenate([pick, pick], axis=1), first, ((1,), (1,))) + dot(pick, last, ((1,), (1,)))
+    result = dot(jnp.concatenate([pick, pick], axis=1), terms, ((1,), (1,)))
     first_lanes = lax.broadcasted_iota(jnp.int32, (size, 128), 1) < 64
     place = lax.rem(lax.broadcasted_iota(jnp.int32, (size, 128), 0), 8) // 2
     for tile in range(rows // 8):
@@ -278,7 +261,8 @@
                 table_sem.at[4 * table + quadrant]))
     loads.append(pltpu.make_async_copy(flips_ref, flips, table_sem.at[8]))
 
-    order = sorted(range(1, groups), key=lambda s: (-(s % gz_count), s))
+    order = sorted(
+        range(1, groups), key=lambda s: (s % gz_count == 0, s < gz_count, abs(s % gz_count - gz_count // 2), -s))
 
     barrier = pltpu.get_barrier_semaphore()
     for step in order:
@@ -523,7 +507,7 @@
     half = depth // 2
     each = half // groups
     forward_table, back_table = depth_tables(depth, groups, each)
-    chunks = rows // 16
+    chunks = rows // 8
     spec_shape = jax.ShapeDtypeStruct((groups, PARTS, rows * 8, cols), f32)
 
     k1, k2, _ = green.shape

time: 112 us -> 111 us (level)
  Pallas kernels: 112 us -> 110 us
where the time goes in v3:
time: 111 us; the launch traced here: 110 us
  Pallas kernels  110 us (99%)
    pallas_call x1, Pallas kernels, fused_plan(): pl.pallas_call(functools.partial(planes_kernel, gy_count, gz_count, reps)...  108 us
    pallas_call x1, Pallas kernels, fused_plan(): pl.pallas_call(depth_out_kernel, out_shape=jax.ShapeDtypeStruct(charges.s...  2.53 us

profile of v3, /device:TPU:0, one launch (start us, length us, event | category | flops | bytes accessed | tf_op | source)
XLA Modules:
  0.0 110.4 jit_solution(10965576090601470597)
XLA Ops:
  0.0 0.0 copy-start
  0.0 107.8 %planes.1.spec_ref = f32[8,2,512,128]{3,2,1,0:T(8,128)S(1)} custom-call(f32[64,128,128]{2,1,0:T(8,128)} %cells_in.1, f32[64,32,128]{2,1,0:T(8,128)} %green_in.1, bf16[512,128]{1,0:T(8,128)(2,1)} %constant.12.clone.pick_in, bf16[256,256]{1,0:T(8,128)(2,1)} %constant.13.clone.depth_table, bf16[3,2,256,256]{3,2,1,0:T(8,128)(2,1)} %constant.10.clone.waves_ref, ...), custom_call_target="tpu_custom_call" | custom-call | tf_op jit(solution)/shard_map/planes/pallas_call | solution.py:530
  107.9 0.0 copy-done
  107.9 2.5 %depth_out.1 = f32[64,128,128]{2,1,0:T(8,128)} custom-call(bf16[256,256]{1,0:T(8,128)(2,1)S(1)} %copy-done, f32[8,2,512,128]{3,2,1,0:T(8,128)S(1)} %planes.1.spec_ref), custom_call_target="tpu_custom_call" | custom-call | tf_op jit(solution)/shard_map/depth_out/pallas_call | solution.py:558
Async XLA Ops:
  0.0 107.9 %copy-start = (bf16[256,256]{1,0:T(8,128)(2,1)S(1)}, bf16[256,256]{1,0:T(8,128)(2,1)}, u32[]{:S(2)}) copy-start(bf16[256,256]{1,0:T(8,128)(2,1)} %constant.14.clone.table_ref) | copy-start | bytes 393220

commit v4 on v3

--- a/solution.py
+++ b/solution.py
@@ -209,14 +209,17 @@
     result = dot(jnp.concatenate([pick, pick], axis=1), terms, ((1,), (1,)))
     first_lanes = lax.broadcasted_iota(jnp.int32, (size, 128), 1) < 64
     place = lax.rem(lax.broadcasted_iota(jnp.int32, (size, 128), 0), 8) // 2
+    even = (place == 0) | (place == 2)
+    stays = first_lanes == even
     for tile in range(rows // 8):
-        spread = []
-        for pair in (2 * tile, 2 * tile + 1):
-            own = result[:size, pair * 128 : (pair + 1) * 128]
-            mirror = result[size:, pair * 128 : (pair + 1) * 128]
-            spread.append(jnp.where(first_lanes, own, pltpu.roll(mirror, 64, 1)))
-            spread.append(jnp.where(first_lanes, pltpu.roll(own, 64, 1), mirror))
-        packed = jnp.where(place < 2, jnp.where(place < 1, spread[0], spread[1]), jnp.where(place < 3, spread[2], spread[3]))
+        own, mirror = (
+            jnp.where(
+                place < 2, result[start : start + size, tile * 256 : tile * 256 + 128],
+                result[start : start + size, tile * 256 + 128 : (tile + 1) * 256])
+            for start in (0, size)
+        )
+        packed = jnp.where(
+            stays, jnp.where(even, own, mirror), pltpu.roll(jnp.where(even, mirror, own), 64, 1))
         out_ref[:, part, :, tile * 8 : (tile + 1) * 8, :] = packed.reshape(groups, halves, 8, 128)
 
 
@@ -224,7 +227,7 @@
     gy_count, gz_count, reps,
     cells_in, green_in, pick_in, depth_table, waves_ref, flips_ref, home_ref,
     cells_ref, field_ref, pick_ref, depth_ref, gains_ref, spec_ref,
-    planes, green, freq, tables, flips,
+    planes, green, freq, waves, tables, flips,
     fwd_send, fwd_recv, back_send, back_recv, green_send, green_recv, right_send, left_send, line_recv, own_sem, table_sem, in_sem,
 ):
     groups = gy_count * gz_count
@@ -251,15 +254,10 @@
     for copy in inputs[:2]:
         copy.start()
 
-    loads = []
-    for table, swap in enumerate((False, True)):
-        minus, plus = (1, 2) if swap else (2, 1)
-        for quadrant, wave in enumerate((0, minus, plus, 0)):
-            loads.append(pltpu.make_async_copy(
-                waves_ref.at[wave],
-                tables.at[table, :, pl.ds(quadrant // 2 * ng, ng), pl.ds(quadrant % 2 * ng, ng)],
-                table_sem.at[4 * table + quadrant]))
-    loads.append(pltpu.make_async_copy(flips_ref, flips, table_sem.at[8]))
+    loads = [
+        pltpu.make_async_copy(source, held, table_sem.at[i])
+        for i, (source, held) in enumerate(((waves_ref, waves), (flips_ref, flips)))
+    ]
 
     order = sorted(
         range(1, groups), key=lambda s: (s % gz_count == 0, s < gz_count, abs(s % gz_count - gz_count // 2), -s))
@@ -353,23 +351,23 @@
     def relay(hop, at):
         @pl.when((rep >= hop) & (rep + 1 < reps))
         def _():
-            line_copy(rep - hop, at, right_send.at[hop], 1).wait_recv()
-            line_copy(rep - hop, at, right_send.at[hop], 1).start()
+            line_copy(rep - hop, at, right_send.at[0], 1).wait_recv()
+            line_copy(rep - hop, at, right_send.at[0], 1).start()
 
         @pl.when((rep + hop < reps) & (rep >= 1))
         def _():
-            line_copy(rep + hop, at, left_send.at[hop], -1).wait_recv()
-            line_copy(rep + hop, at, left_send.at[hop], -1).start()
+            line_copy(rep + hop, at, left_send.at[0], -1).wait_recv()
+            line_copy(rep + hop, at, left_send.at[0], -1).start()
 
     def line_end(at):
         for hop in range(1, reps):
             @pl.when(rep + 1 == reps)
             def _():
-                line_copy(rep - hop, at, right_send.at[hop], 1).wait_recv()
+                line_copy(rep - hop, at, right_send.at[0], 1).wait_recv()
 
             @pl.when(rep == 0)
             def _():
-                line_copy(rep + hop, at, left_send.at[hop], -1).wait_recv()
+                line_copy(rep + hop, at, left_send.at[0], -1).wait_recv()
 
     def load_plane(part, row):
         bands = []
@@ -395,7 +393,7 @@
         return dot(high, flips[...]) + dot(low, flips[...])
 
     def backward(part, half):
-        def body(p, carry):
+        def body(p):
             row = half * 2 + p
             plane = part * 4 + row
             own, mirror = [], []
@@ -406,21 +404,28 @@
                 mirror.append(jnp.where(lane < 64, pltpu.roll(one, 64, 1), two))
             own = jnp.concatenate(own, axis=1).T
             mirror = jnp.concatenate(mirror, axis=1).T
-            packed = (slot == 0) & (plane == 0)
-
-            @pl.when(jnp.logical_not(packed))
-            def _():
+
+            def plain():
                 gain = 0.5 * (own + reflect_plane(mirror))
                 freq[plane] = freq[plane] * jnp.concatenate([gain, gain], axis=0)
 
-            @pl.when(packed)
-            def _():
-                first = 0.5 * (own + reflect_plane(own))
-                second = 0.5 * (mirror + reflect_plane(mirror))
-                mean, odd = 0.5 * (first + second), 0.5 * (first - second)
-                real, imag = freq[plane, :ng, :], freq[plane, ng:, :]
-                freq[plane, :ng, :] = real * mean + reflect_plane(real) * odd
-                freq[plane, ng:, :] = imag * mean - reflect_plane(imag) * odd
+            if plane == 0:
+                packed = slot == 0
+
+                @pl.when(jnp.logical_not(packed))
+                def _():
+                    plain()
+
+                @pl.when(packed)
+                def _():
+                    first = 0.5 * (own + reflect_plane(own))
+                    second = 0.5 * (mirror + reflect_plane(mirror))
+                    mean, odd = 0.5 * (first + second), 0.5 * (first - second)
+                    real, imag = freq[plane, :ng, :], freq[plane, ng:, :]
+                    freq[plane, :ng, :] = real * mean + reflect_plane(real) * odd
+                    freq[plane, ng:, :] = imag * mean - reflect_plane(imag) * odd
+            else:
+                plain()
 
             undo = table_dot(tables[0, 0], tables[0, 1], freq[plane])
             undo = jnp.concatenate([undo[:ng], undo[ng:]], axis=1)
@@ -431,11 +436,11 @@
                     for x in range(gz_count):
                         planes[y * gz_count + x, part, pl.ds(c * 4 + row, rows, stride=8), :] = cells[
                             x * rows : (x + 1) * rows, c * ng + y * cols : c * ng + (y + 1) * cols]
-            return carry
-
-        lax.fori_loop(0, 2, body, 0)
-
-    own_home = [pltpu.make_async_copy(planes.at[slot, h], home_ref.at[slot, h], own_sem.at[h]) for h in range(PARTS)]
+
+        for p in range(2):
+            body(p)
+
+    own_home = [pltpu.make_async_copy(planes.at[slot, h], home_ref.at[slot, h], own_sem.at[0]) for h in range(PARTS)]
 
     def arrive(part):
         whole(planes.at[others, part], fwd_recv.at[part]).wait_recv()
@@ -448,9 +453,9 @@
 
     first, second = quarters[:HALVES], quarters[HALVES:]
 
-    def second_start(hop):
-        for at in second:
-            line_start(at, hop)
+    def second_relay(hop):
+        relay(hop, second[0])
+        line_start(second[1], hop)
 
     for at in first:
         green_wait(at)
@@ -458,25 +463,32 @@
     relay(1, first[0])
     for at in second:
         green_wait(at)
-    second_start(0)
+    for at in second:
+        line_start(at, 0)
     relay(1, first[1])
-    second_start(1)
+    line_start(second[0], 1)
     for hop in range(2, reps - 1):
         for at in first:
             relay(hop, at)
-        second_start(hop)
+        line_start(second[0], hop)
     for load in loads:
         load.wait()
-    relay(1, second[0])
+    for table, swap in enumerate((False, True)):
+        minus, plus = (1, 2) if swap else (2, 1)
+        for quadrant, wave in enumerate((0, minus, plus, 0)):
+            down, right = quadrant // 2 * ng, quadrant % 2 * ng
+            tables[table, :, down : down + ng, right : right + ng] = waves[wave]
+    second_relay(1)
     arrive(0)
-    relay(1, second[1])
     for at in first:
         line_end(at)
         backward(*at)
-        if at == first[-1]:
-            depart(0)
-        for hop in range(2, reps - 1):
-            relay(hop, second[at[1]])
+        if at == first[0]:
+            for hop in range(2, reps - 1):
+                second_relay(hop)
+    depart(0)
+    for hop in range(1, reps - 1):
+        relay(hop, second[1])
     arrive(1)
     for at in second:
         line_end(at)
@@ -485,16 +497,15 @@
 
     whole(gains_ref.at[others], green_send.at[0]).wait_send()
     whole(spec_ref.at[others], fwd_send.at[0]).wait_send()
-    for hop in range(reps):
-        @pl.when((rep >= hop) & (rep + 1 < reps))
+    for at in range(1, reps):
+        @pl.when(rep + 1 == at)
         def _():
-            whole(green.at[rep - hop], right_send.at[hop]).wait_send()
-
-        @pl.when((rep + hop < reps) & (rep >= 1))
+            whole(green.at[pl.ds(0, at)], right_send.at[0]).wait_send()
+
+        @pl.when(rep == at)
         def _():
-            whole(green.at[rep + hop], left_send.at[hop]).wait_send()
-    for part in range(PARTS):
-        own_home[part].wait()
+            whole(green.at[pl.ds(at, reps - at)], left_send.at[0]).wait_send()
+    pltpu.make_async_copy(planes.at[slot], home_ref.at[slot], own_sem.at[0]).wait()
     whole(planes.at[others], back_send.at[0]).wait_send()
     whole(home_ref.at[others], back_recv.at[0]).wait_recv()
 
@@ -541,10 +552,11 @@
             pltpu.VMEM(spec_shape.shape, f32),
             pltpu.VMEM((reps, PARTS, HALVES, ng * 2, 2 * k1), f32),
             pltpu.VMEM((each, 2 * ng, ng), f32),
+            pltpu.VMEM(waves.shape, bf16),
             pltpu.VMEM((2, 2, 2 * ng, 2 * ng), bf16),
             pltpu.VMEM((ng, ng), bf16),
             dma((1,)), dma((PARTS,)), dma((1,)), dma((1,)), dma((1,)), dma((PARTS, HALVES)),
-            dma((reps,)), dma((reps,)), dma((reps, PARTS, HALVES)), dma((PARTS,)), dma((9,)), dma((4,)),
+            dma((1,)), dma((1,)), dma((reps, PARTS, HALVES)), dma((1,)), dma((2,)), dma((4,)),
         ],
         compiler_params=pltpu.CompilerParams(
             collective_id=0, has_side_effects=True, vmem_limit_bytes=44 * 2**20),

time: 111 us -> 110 us (level)
  no operation moved by 1% of the time
where the time goes in v4:
time: 110 us
  Pallas kernels  109 us (99%)
    pallas_call x1, Pallas kernels, fused_plan(): pl.pallas_call(functools.partial(planes_kernel, gy_count, gz_count, reps)...  107 us
    pallas_call x1, Pallas kernels, fused_plan(): pl.pallas_call(depth_out_kernel, out_shape=jax.ShapeDtypeStruct(charges.s...  2.53 us

profile of v4, /device:TPU:0, one launch (start us, length us, event | category | flops | bytes accessed | tf_op | source)
XLA Modules:
  0.0 109.7 jit_solution(747303135893531256)
XLA Ops:
  0.0 0.0 copy-start
  0.0 106.9 %planes.1.spec_ref = f32[8,2,512,128]{3,2,1,0:T(8,128)S(1)} custom-call(f32[64,128,128]{2,1,0:T(8,128)} %cells_in.1, f32[64,32,128]{2,1,0:T(8,128)} %green_in.1, bf16[512,128]{1,0:T(8,128)(2,1)} %constant.12.clone.pick_in, bf16[256,256]{1,0:T(8,128)(2,1)} %constant.13.clone.depth_table, bf16[3,2,256,256]{3,2,1,0:T(8,128)(2,1)} %constant.10.clone.waves_ref, ...), custom_call_target="tpu_custom_call" | custom-call | tf_op jit(solution)/shard_map/planes/pallas_call | solution.py:541
  107.0 0.0 copy-done
  107.0 2.5 %depth_out.1 = f32[64,128,128]{2,1,0:T(8,128)} custom-call(bf16[256,256]{1,0:T(8,128)(2,1)S(1)} %copy-done, f32[8,2,512,128]{3,2,1,0:T(8,128)S(1)} %planes.1.spec_ref), custom_call_target="tpu_custom_call" | custom-call | tf_op jit(solution)/shard_map/depth_out/pallas_call | solution.py:570
Async XLA Ops:
  0.0 107.0 %copy-start = (bf16[256,256]{1,0:T(8,128)(2,1)S(1)}, bf16[256,256]{1,0:T(8,128)(2,1)}, u32[]{:S(2)}) copy-start(bf16[256,256]{1,0:T(8,128)(2,1)} %constant.14.clone.table_ref) | copy-start | bytes 393220

commit v5 on v4

--- a/solution.py
+++ b/solution.py
@@ -251,8 +251,6 @@
         for i, (source, held) in enumerate((
             (green_in, field_ref.at[:, pl.ds(0, green_in.shape[1]), :]), (pick_in, pick_ref), (cells_in, cells_ref), (depth_table, depth_ref)))
     ]
-    for copy in inputs[:2]:
-        copy.start()
 
     loads = [
         pltpu.make_async_copy(source, held, table_sem.at[i])
@@ -274,6 +272,8 @@
     def _():
         pl.semaphore_signal(barrier, inc=1, device_id=along(-1), device_id_type=MESH)
 
+    for copy in inputs[:2]:
+        copy.start()
     for copy in inputs[:2]:
         copy.wait()
     for copy in inputs[2:]:

time: 110 us -> 110 us (level)
  no operation moved by 1% of the time
where the time goes in v5:
time: 110 us
  Pallas kernels  110 us (100%)
    pallas_call x1, Pallas kernels, fused_plan(): pl.pallas_call(functools.partial(planes_kernel, gy_count, gz_count, reps)...  107 us
    pallas_call x1, Pallas kernels, fused_plan(): pl.pallas_call(depth_out_kernel, out_shape=jax.ShapeDtypeStruct(charges.s...  2.53 us

profile of v5, /device:TPU:0, one launch (start us, length us, event | category | flops | bytes accessed | tf_op | source)
XLA Modules:
  0.0 109.7 jit_solution(2922095488509746338)
XLA Ops:
  0.0 0.0 copy-start
  0.0 107.0 %planes.1.spec_ref = f32[8,2,512,128]{3,2,1,0:T(8,128)S(1)} custom-call(f32[64,128,128]{2,1,0:T(8,128)} %cells_in.1, f32[64,32,128]{2,1,0:T(8,128)} %green_in.1, bf16[512,128]{1,0:T(8,128)(2,1)} %constant.12.clone.pick_in, bf16[256,256]{1,0:T(8,128)(2,1)} %constant.13.clone.depth_table, bf16[3,2,256,256]{3,2,1,0:T(8,128)(2,1)} %constant.10.clone.waves_ref, ...), custom_call_target="tpu_custom_call" | custom-call | tf_op jit(solution)/shard_map/planes/pallas_call | solution.py:541
  107.0 0.0 copy-done
  107.0 2.5 %depth_out.1 = f32[64,128,128]{2,1,0:T(8,128)} custom-call(bf16[256,256]{1,0:T(8,128)(2,1)S(1)} %copy-done, f32[8,2,512,128]{3,2,1,0:T(8,128)S(1)} %planes.1.spec_ref), custom_call_target="tpu_custom_call" | custom-call | tf_op jit(solution)/shard_map/depth_out/pallas_call | solution.py:570
Async XLA Ops:
  0.0 107.0 %copy-start = (bf16[256,256]{1,0:T(8,128)(2,1)S(1)}, bf16[256,256]{1,0:T(8,128)(2,1)}, u32[]{:S(2)}) copy-start(bf16[256,256]{1,0:T(8,128)(2,1)} %constant.14.clone.table_ref) | copy-start | bytes 393220
